TPU v7x, 32 devices: a whole 2x2x4 slice. The times are simulated.
32 devices in a mesh: band: 8 (over z, x), gvec: 4 (over y, core).
Axes of the slice: x: 2, y: 2, z: 4, core: 2. Of those that a mesh axis runs over, the one named last changes fastest.
Arguments:
- wave_coeffs: bfloat16 [2, 256, 75264], P(None, 'band', 'gvec'), may hold values from -6 to 6
- projectors: bfloat16 [2, 64, 75264], P(None, 'band', 'gvec'), may hold values from -0.0234375 to 0.0234375
- miller_index: int32 [3, 75264], P(None, 'gvec'), may hold values from -24 to 24
- lattice: float32 [3, 3], replicated, may hold values from -0.25 to 1.25
- occupation: float32 [256], P('band'), may hold values from 0 to 2
- species: int32 [8], replicated, may hold values from 0 to 3
- proj_count: int32 [8], replicated, may hold values from 4 to 8
- coupling: float32 [4, 8, 8], replicated, may hold values from -0.4 to 2, as said below
Outputs:
- forces: float32 [3, 8], P(None, 'band')
- stress: float32 [3, 3], replicated
Inputs may be any that keep to these rules, and one draw needn't show every extreme that they name: `coupling`: symmetric in its last two dimensions.
All inputs are finite; a program needn't handle non-finite values.
Results may differ from a plain program's by a relative error of at most 0.006.
Values may be sent and summed in bfloat16 or wider, within the bound.
A program may use at most 64 MiB of HBM per device.

v0:
```python
import math
import jax
import jax.numpy as jnp
from jax import lax
from jax.sharding import PartitionSpec as P

PROJ = 8
MILLER = 24
stress_pairs = ((0, 0), (1, 1), (2, 2), (0, 1), (0, 2), (1, 2))


def cart_weights(miller_index, lattice):
    indices = miller_index.astype(jnp.float32)
    coords = []
    for column in range(3):
        coords.append(
            (
                indices[0] * lattice[0, column]
                + indices[1] * lattice[1, column]
                + indices[2] * lattice[2, column]
            )
            / MILLER
        )
    isotropic = (coords[0] * coords[0] + coords[1] * coords[1] + coords[2] * coords[2]) / 3.0
    weight_rows = [jnp.ones_like(coords[0])] + coords
    for first_axis, second_axis in stress_pairs:
        product = coords[first_axis] * coords[second_axis]
        if first_axis == second_axis:
            product = product - isotropic
        weight_rows.append(product)
    return jnp.stack(weight_rows)


def scale_block(weights, atom_block):
    proj_rows = atom_block.shape[1]
    scaled = (weights[:, None, None, :] * atom_block[None].astype(jnp.float32)).astype(jnp.bfloat16)
    return scaled.reshape(20 * proj_rows, atom_block.shape[2])


def intersection(scaled, flat_waves):
    product = lax.dot_general(
        scaled, flat_waves, (((1,), (1,)), ((), ())), preferred_element_type=jnp.float32
    )
    product = product.reshape(10, 2, scaled.shape[0] // 20, 2, flat_waves.shape[0] // 2)
    real_part = product[:, 0, :, 0] + product[:, 1, :, 1]
    imag_part = product[:, 0, :, 1] - product[:, 1, :, 0]
    return jnp.stack([real_part, imag_part], axis=1)


def atom_couplings(species, proj_count, coupling):
    kind_count = coupling.shape[0]
    proj_width = coupling.shape[1]
    onehot = (species[:, None] == jnp.arange(kind_count, dtype=jnp.int32)[None, :]).astype(
        jnp.float32
    )
    chosen = jnp.einsum("as,sij->aij", onehot, coupling, precision=lax.Precision.HIGHEST)
    active = (jnp.arange(proj_width, dtype=jnp.int32)[None, :] < proj_count[:, None]).astype(
        jnp.float32
    )
    return chosen * active[:, :, None] * active[:, None, :]


def contract(per_atom, couplings, occupied):
    mixed = jnp.einsum("aij,kcajn->kcain", couplings, per_atom, precision=lax.Precision.HIGHEST)
    becp_real = per_atom[0, 0]
    becp_imag = per_atom[0, 1]
    imag_sum = jnp.sum(becp_real[None] * mixed[1:4, 1] - becp_imag[None] * mixed[1:4, 0], axis=2)
    real_sum = jnp.sum(becp_real[None] * mixed[4:, 0] + becp_imag[None] * mixed[4:, 1], axis=2)
    force_part = jnp.sum(imag_sum * occupied, axis=2)
    stress_part = jnp.sum(real_sum * occupied, axis=(1, 2))
    return (force_part, stress_part)


def stress_matrix(values):
    return jnp.stack(
        [
            jnp.stack([values[0], values[3], values[4]]),
            jnp.stack([values[3], values[1], values[5]]),
            jnp.stack([values[4], values[5], values[2]]),
        ]
    )


def body(wave_coeffs, projectors, miller_index, lattice, occupation, species, proj_count, coupling):
    weights = cart_weights(miller_index, lattice)
    band_count = wave_coeffs.shape[1]
    quarter_count = band_count // lax.axis_size("gvec")
    group_slot = lax.axis_index("gvec")
    atom_total = species.shape[0]
    flat_waves = wave_coeffs.reshape(2 * band_count, wave_coeffs.shape[2])
    total_proj = PROJ * lax.axis_size("band")
    start_carry = jnp.zeros((band_count, 10, 2, total_proj), jnp.float32)
    arrived = lax.all_gather(projectors, "band", axis=1, tiled=True)
    block_rows = arrived.shape[1]
    anchor = jnp.zeros((), jnp.int32)

    def one_atom(atom_slot, partial_value):
        atom_block = lax.dynamic_slice_in_dim(arrived, atom_slot * PROJ, PROJ, 1)
        values = intersection(scale_block(weights, atom_block), flat_waves).transpose(3, 0, 1, 2)
        return lax.dynamic_update_slice(
            partial_value, values, (anchor, anchor, anchor, atom_slot * PROJ)
        )

    intersections = lax.fori_loop(0, block_rows // PROJ, one_atom, start_carry)
    couplings = atom_couplings(species, proj_count, coupling)
    owned_rows = lax.psum_scatter(intersections, "gvec", scatter_dimension=0, tiled=True)
    occupied = lax.dynamic_slice_in_dim(occupation, group_slot * quarter_count, quarter_count, 0)
    per_atom = owned_rows.reshape(quarter_count, 10, 2, atom_total, PROJ).transpose(1, 2, 3, 4, 0)
    force_part, stress_part = contract(per_atom, couplings, occupied)
    band_total = band_count * lax.axis_size("band")
    force_scale = 2.0 / (PROJ * math.sqrt(band_total))
    stress_scale = 1.0 / (PROJ * math.sqrt(atom_total * band_total))
    all_force, total_stress = lax.psum((force_part, stress_part), ("band", "gvec"))
    owned_atoms = atom_total // lax.axis_size("band")
    own_force = lax.dynamic_slice_in_dim(
        all_force, lax.axis_index("band") * owned_atoms, owned_atoms, 1
    )
    return (own_force * force_scale, stress_matrix(total_stress * stress_scale))


def solution(mesh):
    return jax.shard_map(
        body,
        mesh=mesh,
        in_specs=(
            P(None, "band", "gvec"),
            P(None, "band", "gvec"),
            P(None, "gvec"),
            P(),
            P("band"),
            P(),
            P(),
            P(),
        ),
        out_specs=(P(None, "band"), P()),
        check_vma=False,
    )
```

profile of v0, /device:TPU:0, one launch (start us, length us, event | category | flops | bytes accessed | tf_op | source)
XLA Modules:
  0.0 217.9 jit_solution(4178742472580967056)
XLA Ops:
  7.2 0.0 copy-start
  7.2 0.0 all-gather.2.cloned.1.call-start
  7.2 0.7 all-gather.2.cloned.1.call-update
  7.9 0.0 all-reduce.4.cloned.1.call-start
  8.0 1.7 fusion.27
  9.7 1.0 convert_element_type.32
  10.7 0.7 fusion.21
  11.4 0.1 copy.31
  11.5 1.2 dynamic-slice
  13.3 0.7 dynamic_slice.13
  14.1 4.2 %fusion.25 = (f32[1,18816]{1,0:T(1,128)S(1)}, f32[1,18816]{1,0:T(1,128)S(1)}, f32[1,18816]{1,0:T(1,128)S(1)}) fusion(f32[]{:T(128)} %bitcast.16, f32[3,18816]{1,0:T(4,128)S(1)} %convert_element_type.32, f32[]{:T(128)} %bitcast.15, f32[]{:T(128)} %bitcast.14, f32[]{:T(128)} %bitcast.13, f32[]{:T(128)} %bitcast.12, f32[]{:T(128)} %bitcast.11), kind=kLoop, calls=%fused_computation.55 | loop fusion | flops 244608 | bytes 451608 | tf_op jit(solution)/shard_map/mul | solution.py:27
  18.3 2.1 fusion.26
  20.4 0.2 multiply_subtract_fusion
  20.6 0.1 multiply_subtract_fusion.1
  20.8 1.3 stack.48
  22.0 71.5 %all-gather.2.cloned.1.call-done = bf16[2,64,18816]{2,1,0:T(8,128)(2,1)} async-done(((bf16[2,8,18816]{2,1,0:T(8,128)(2,1)}), bf16[2,64,18816]{2,1,0:T(8,128)(2,1)}) %all-gather.2.cloned.1.call-update) | async-done | bytes 4816912 | tf_op jit(solution)/shard_map/all_gather | solution.py:93
  93.5 0.1 broadcast_in_dim.8
  93.6 0.0 copy-start.1
  93.6 37.3 %while.13 = (s32[]{:T(128)}, f32[32,10,2,64]{0,3,1,2:T(8,128)S(1)}, f32[10,18816]{1,0:T(8,128)S(1)}, bf16[2,64,18816]{2,1,0:T(8,128)(2,1)}, bf16[64,18816]{1,0:T...) while((s32[]{:T(128)}, f32[32,10,2,64]{0,3,1,2:T(8,128)S(1)}, f32[10,18816]{1,0:T(8,128)S(1)}, ...), condition=%wide.region_1.0_spmd, body=%wide.region_0.0_spmd.sunk | while | flops 391684096 | bytes 6438035 | solution.py:104
  93.6 1.2 dynamic-slice_convert_fusion.2
  94.8 3.4 %fusion.40 = f32[10,2,8,2,32]{4,2,3,1,0:T(8,128)S(1)} fusion(bf16[2,32,18816,1,1]{2,1,0,4,3:T(8,128)(2,1)} %bitcast.110, f32[2,8,18816]{2,1,0:T(8,128)S(1)} %dynamic-slice_convert_fusion.2, f32[10,18816]{1,0:T(8,128)S(1)} %get-tuple-element.190), kind=kOutput, calls=%fused_computation.2.clone.1 | convolution fusion | flops 391372800 | bytes 4406272 | tf_op jit(solution)/shard_map/while/body/eval_jaxpr/dot_general | solution.py:41
  98.3 1.2 dynamic-slice_convert_fusion.2
  99.4 3.4 %fusion.40 = f32[10,2,8,2,32]{4,2,3,1,0:T(8,128)S(1)} fusion(bf16[2,32,18816,1,1]{2,1,0,4,3:T(8,128)(2,1)} %bitcast.110, f32[2,8,18816]{2,1,0:T(8,128)S(1)} %dynamic-slice_convert_fusion.2, f32[10,18816]{1,0:T(8,128)S(1)} %get-tuple-element.190), kind=kOutput, calls=%fused_computation.2.clone.1 | convolution fusion | flops 391372800 | bytes 4406272 | tf_op jit(solution)/shard_map/while/body/eval_jaxpr/dot_general | solution.py:41
  102.9 1.2 dynamic-slice_convert_fusion.2
  104.1 3.4 %fusion.40 = f32[10,2,8,2,32]{4,2,3,1,0:T(8,128)S(1)} fusion(bf16[2,32,18816,1,1]{2,1,0,4,3:T(8,128)(2,1)} %bitcast.110, f32[2,8,18816]{2,1,0:T(8,128)S(1)} %dynamic-slice_convert_fusion.2, f32[10,18816]{1,0:T(8,128)S(1)} %get-tuple-element.190), kind=kOutput, calls=%fused_computation.2.clone.1 | convolution fusion | flops 391372800 | bytes 4406272 | tf_op jit(solution)/shard_map/while/body/eval_jaxpr/dot_general | solution.py:41
  107.6 1.2 dynamic-slice_convert_fusion.2
  108.7 3.4 %fusion.40 = f32[10,2,8,2,32]{4,2,3,1,0:T(8,128)S(1)} fusion(bf16[2,32,18816,1,1]{2,1,0,4,3:T(8,128)(2,1)} %bitcast.110, f32[2,8,18816]{2,1,0:T(8,128)S(1)} %dynamic-slice_convert_fusion.2, f32[10,18816]{1,0:T(8,128)S(1)} %get-tuple-element.190), kind=kOutput, calls=%fused_computation.2.clone.1 | convolution fusion | flops 391372800 | bytes 4406272 | tf_op jit(solution)/shard_map/while/body/eval_jaxpr/dot_general | solution.py:41
  112.2 1.2 dynamic-slice_convert_fusion.2
  113.4 3.4 %fusion.40 = f32[10,2,8,2,32]{4,2,3,1,0:T(8,128)S(1)} fusion(bf16[2,32,18816,1,1]{2,1,0,4,3:T(8,128)(2,1)} %bitcast.110, f32[2,8,18816]{2,1,0:T(8,128)S(1)} %dynamic-slice_convert_fusion.2, f32[10,18816]{1,0:T(8,128)S(1)} %get-tuple-element.190), kind=kOutput, calls=%fused_computation.2.clone.1 | convolution fusion | flops 391372800 | bytes 4406272 | tf_op jit(solution)/shard_map/while/body/eval_jaxpr/dot_general | solution.py:41
  116.9 1.2 dynamic-slice_convert_fusion.2
  118.1 3.4 %fusion.40 = f32[10,2,8,2,32]{4,2,3,1,0:T(8,128)S(1)} fusion(bf16[2,32,18816,1,1]{2,1,0,4,3:T(8,128)(2,1)} %bitcast.110, f32[2,8,18816]{2,1,0:T(8,128)S(1)} %dynamic-slice_convert_fusion.2, f32[10,18816]{1,0:T(8,128)S(1)} %get-tuple-element.190), kind=kOutput, calls=%fused_computation.2.clone.1 | convolution fusion | flops 391372800 | bytes 4406272 | tf_op jit(solution)/shard_map/while/body/eval_jaxpr/dot_general | solution.py:41
  121.6 1.2 dynamic-slice_convert_fusion.2
  122.7 3.4 %fusion.40 = f32[10,2,8,2,32]{4,2,3,1,0:T(8,128)S(1)} fusion(bf16[2,32,18816,1,1]{2,1,0,4,3:T(8,128)(2,1)} %bitcast.110, f32[2,8,18816]{2,1,0:T(8,128)S(1)} %dynamic-slice_convert_fusion.2, f32[10,18816]{1,0:T(8,128)S(1)} %get-tuple-element.190), kind=kOutput, calls=%fused_computation.2.clone.1 | convolution fusion | flops 391372800 | bytes 4406272 | tf_op jit(solution)/shard_map/while/body/eval_jaxpr/dot_general | solution.py:41
  126.2 1.2 dynamic-slice_convert_fusion.2
  127.4 3.4 %fusion.40 = f32[10,2,8,2,32]{4,2,3,1,0:T(8,128)S(1)} fusion(bf16[2,32,18816,1,1]{2,1,0,4,3:T(8,128)(2,1)} %bitcast.110, f32[2,8,18816]{2,1,0:T(8,128)S(1)} %dynamic-slice_convert_fusion.2, f32[10,18816]{1,0:T(8,128)S(1)} %get-tuple-element.190), kind=kOutput, calls=%fused_computation.2.clone.1 | convolution fusion | flops 391372800 | bytes 4406272 | tf_op jit(solution)/shard_map/while/body/eval_jaxpr/dot_general | solution.py:41
  130.9 1.0 copy.27
  131.8 0.0 all-reduce.4.cloned.1.call-update
  131.9 0.0 copy-done
  131.9 0.0 copy-done.1
  131.9 0.2 fusion.10
  132.1 30.9 %all-reduce.4.cloned.1.call-done = f32[32,10,2,64]{3,2,1,0:T(2,128)} async-done(((f32[32,10,2,64]{3,2,1,0:T(2,128)}), f32[32,10,2,64]{3,2,1,0:T(2,128)}) %all-reduce.4.cloned.1.call-update) | async-done | bytes 163856
  162.9 0.9 constant_dynamic-slice_fusion
  163.8 0.3 copy.28
  164.1 0.8 copy.32
  164.9 0.1 copy.29
  165.0 0.1 copy.35
  165.1 0.6 convolution_bitcast_fusion
  165.7 0.4 fusion.13
  166.0 0.4 fusion.17
  166.4 0.1 multiply_reduce_fusion
  166.5 0.1 multiply_reduce_fusion.1
  166.6 39.4 %all-reduce.1 = (f32[3,8]{0,1:T(8,128)S(1)}, f32[6]{0:T(128)S(1)}) all-reduce(f32[3,8]{0,1:T(8,128)S(1)} %multiply_reduce_fusion.1, f32[6]{0:T(128)S(1)} %multiply_reduce_fusion), channel_id=1, replica_groups=mesh['band'=8,'gvec'=4] {'band','gvec'}, use_global_device_ids=true, to_apply=%region_5.0 | all-reduce | flops 30 | bytes 240 | tf_op jit(solution)/shard_map/psum | solution.py:113
  205.9 0.7 fusion.28
  206.6 0.1 fusion.29
  206.7 0.7 maximum_bitcast_fusion.3
  207.4 0.5 dynamic-slice_multiply_fusion
  207.9 2.6 %maximum_bitcast_fusion.1 = (f32[1,3]{1,0:T(1,128)S(1)}, f32[1,3]{1,0:T(1,128)S(1)}) fusion(f32[2]{0:T(128)S(1)} %get-tuple-element.135, f32[1]{0:T(128)} %get-tuple-element.130, f32[1]{0:T(128)} %get-tuple-element.132, f32[1]{0:T(128)} %get-tuple-element.133, f32[1]{0:T(128)} %get-tuple-element.134), kind=kLoop, calls=%fused_computation.49 | loop fusion | flops 9 | bytes 48 | tf_op jit(solution)/shard_map/stack | solution.py:75
  210.5 0.6 pad_maximum_fusion
  (27 shorter events, 0.3 us)
Async XLA Ops:
  7.2 124.7 %copy-start = (f32[4,8,8]{2,1,0:T(8,128)S(1)}, f32[4,8,8]{2,1,0:T(8,128)}, u32[]{:S(2)}) copy-start(f32[4,8,8]{2,1,0:T(8,128)} %param.17) | copy-start | bytes 3076
  7.2 86.3 %all-gather.2.cloned.1.call-start = ((), (), s32[]{:S(2)}) async-start(), calls=%async_computation | async-start | bytes 5419008 | tf_op jit(solution)/shard_map/all_gather | solution.py:93
  7.9 155.0 %all-reduce.4.cloned.1.call-start = ((), (), s32[]{:S(2)}) async-start(), calls=%async_computation.1 | async-start | bytes 655360
  93.6 38.3 %copy-start.1 = (s32[8]{0:T(128)S(1)}, s32[8]{0:T(128)}, u32[]{:S(2)}) copy-start(s32[8]{0:T(128)} %param.15) | copy-start | bytes 100
Sparse Core Ops, SparseCore 0:
  10.2 83.2 all-gather.1
  132.0 30.9 all-reduce.3
where the time goes:
time: 219 us; the launch traced here: 218 us
  waiting for transfers between devices  103 us (47%)
  blocking collectives  39.4 us (18%)
  matrix products  28.2 us (13%)
  other arithmetic  23.1 us (11%)
  between operations  14.8 us (7%)
  local copies, waits for them, and re-layouts  8.95 us (4%)
    all_gather x1, waiting for transfers between devices, body(): arrived = lax.all_gather(projectors, 'band', axis=1, tiled=True)  71.5 us
    psum x1, blocking collectives, body(): lax.psum((force_part, stress_part), ('band', 'gvec'))  39.4 us
    unnamed x3, waiting for transfers between devices  31.5 us
    dot_general x8, matrix products, intersection(): lax.dot_general(scaled, flat_waves, (((1,), (1,)), ((), ())), preferred_e...  27.4 us
    convert_element_type x8, other arithmetic, scale_block(): atom_block[None].astype(jnp.float32)  9.23 us
    mul x2, other arithmetic, cart_weights(): product = coords[first_axis] * coords[second_axis]  6.28 us
  transfers between devices with their start and end apart: 2, of which 2 were waited for; matrix products, arithmetic and copies ran while one was open for 6% of the time, Pallas kernels for 0%

commit v1 on v0

--- a/solution.py
+++ b/solution.py
@@ -110,7 +110,7 @@
     band_total = band_count * lax.axis_size("band")
     force_scale = 2.0 / (PROJ * math.sqrt(band_total))
     stress_scale = 1.0 / (PROJ * math.sqrt(atom_total * band_total))
-    all_force, total_stress = lax.psum((force_part, stress_part), ("band", "gvec"))
+    all_force, total_stress = lax.psum(lax.psum((force_part, stress_part), "gvec"), "band")
     owned_atoms = atom_total // lax.axis_size("band")
     own_force = lax.dynamic_slice_in_dim(
         all_force, lax.axis_index("band") * owned_atoms, owned_atoms, 1

time: 219 us -> 207 us (0.945)
  blocking collectives: 39.4 us -> 27.6 us
    psum x1 -> x2, blocking collectives: 39.4 us -> 27.6 us  [the longest x1 21.8 us: body(): lax.psum(lax.psum((force_part, stress_part), 'gvec'), 'band')]
  transfers between devices with their start and end apart: 2 -> 2, of which waited for: 2 -> 2; matrix products, arithmetic and copies ran while one was open for 6% -> 7% of each run, Pallas kernels for 0% -> 0%
where the time goes in v1:
time: 207 us; the launch traced here: 206 us
  waiting for transfers between devices  103 us (50%)
  matrix products  28.2 us (14%)
  blocking collectives  27.6 us (13%)
  other arithmetic  23.1 us (11%)
  between operations  14.8 us (7%)
  local copies, waits for them, and re-layouts  8.98 us (4%)
    all_gather x1, waiting for transfers between devices, body(): arrived = lax.all_gather(projectors, 'band', axis=1, tiled=True)  71.4 us
    unnamed x3, waiting for transfers between devices  31.6 us
    dot_general x8, matrix products, intersection(): lax.dot_general(scaled, flat_waves, (((1,), (1,)), ((), ())), preferred_e...  27.4 us
    psum x1, blocking collectives, body(): lax.psum(lax.psum((force_part, stress_part), 'gvec'), 'band')  21.8 us
    convert_element_type x8, other arithmetic, scale_block(): atom_block[None].astype(jnp.float32)  9.23 us
    mul x2, other arithmetic, cart_weights(): product = coords[first_axis] * coords[second_axis]  6.28 us
    psum x1, blocking collectives, body(): lax.psum((force_part, stress_part), 'gvec')  5.85 us
  transfers between devices with their start and end apart: 2, of which 2 were waited for; matrix products, arithmetic and copies ran while one was open for 7% of the time, Pallas kernels for 0%

profile of v1, /device:TPU:0, one launch (start us, length us, event | category | flops | bytes accessed | tf_op | source)
XLA Modules:
  0.0 206.2 jit_solution(15706976014731857109)
XLA Ops:
  7.2 0.0 copy-start
  7.2 0.0 all-gather.2.cloned.1.call-start
  7.2 0.7 all-gather.2.cloned.1.call-update
  7.9 0.0 all-reduce.5.cloned.1.call-start
  8.0 1.7 fusion.27
  9.7 1.0 convert_element_type.32
  10.7 0.7 fusion.21
  11.4 0.1 copy.31
  11.5 1.3 dynamic-slice
  13.4 0.7 dynamic_slice.13
  14.1 4.2 %fusion.25 = (f32[1,18816]{1,0:T(1,128)S(1)}, f32[1,18816]{1,0:T(1,128)S(1)}, f32[1,18816]{1,0:T(1,128)S(1)}) fusion(f32[]{:T(128)} %bitcast.16, f32[3,18816]{1,0:T(4,128)S(1)} %convert_element_type.32, f32[]{:T(128)} %bitcast.15, f32[]{:T(128)} %bitcast.14, f32[]{:T(128)} %bitcast.13, f32[]{:T(128)} %bitcast.12, f32[]{:T(128)} %bitcast.11), kind=kLoop, calls=%fused_computation.55 | loop fusion | flops 244608 | bytes 451608 | tf_op jit(solution)/shard_map/mul | solution.py:27
  18.3 2.1 %fusion.26 = (f32[1,18816]{1,0:T(1,128)S(1)}, f32[1,18816]{1,0:T(1,128)S(1)}) fusion(f32[1,18816]{1,0:T(1,128)S(1)} %get-tuple-element.112, f32[]{:T(128)} %bitcast.10, f32[3,18816]{1,0:T(4,128)S(1)} %convert_element_type.32, f32[]{:T(128)} %bitcast.9, f32[]{:T(128)} %bitcast.8), kind=kLoop, calls=%fused_computation.56 | loop fusion | flops 131712 | bytes 451596 | tf_op jit(solution)/shard_map/mul | solution.py:27
  20.4 0.2 multiply_subtract_fusion
  20.6 0.1 multiply_subtract_fusion.1
  20.8 1.3 stack.48
  22.1 71.4 %all-gather.2.cloned.1.call-done = bf16[2,64,18816]{2,1,0:T(8,128)(2,1)} async-done(((bf16[2,8,18816]{2,1,0:T(8,128)(2,1)}), bf16[2,64,18816]{2,1,0:T(8,128)(2,1)}) %all-gather.2.cloned.1.call-update) | async-done | bytes 4816912 | tf_op jit(solution)/shard_map/all_gather | solution.py:93
  93.5 0.1 broadcast_in_dim.8
  93.6 0.0 copy-start.1
  93.6 37.3 %while.13 = (s32[]{:T(128)}, f32[32,10,2,64]{0,3,1,2:T(8,128)S(1)}, f32[10,18816]{1,0:T(8,128)S(1)}, bf16[2,64,18816]{2,1,0:T(8,128)(2,1)}, bf16[64,18816]{1,0:T...) while((s32[]{:T(128)}, f32[32,10,2,64]{0,3,1,2:T(8,128)S(1)}, f32[10,18816]{1,0:T(8,128)S(1)}, ...), condition=%wide.region_1.0_spmd, body=%wide.region_0.0_spmd.sunk | while | flops 391684096 | bytes 6438035 | solution.py:104
  93.6 1.2 dynamic-slice_convert_fusion.2
  94.8 3.4 %fusion.40 = f32[10,2,8,2,32]{4,2,3,1,0:T(8,128)S(1)} fusion(bf16[2,32,18816,1,1]{2,1,0,4,3:T(8,128)(2,1)} %bitcast.110, f32[2,8,18816]{2,1,0:T(8,128)S(1)} %dynamic-slice_convert_fusion.2, f32[10,18816]{1,0:T(8,128)S(1)} %get-tuple-element.192), kind=kOutput, calls=%fused_computation.2.clone.1 | convolution fusion | flops 391372800 | bytes 4406272 | tf_op jit(solution)/shard_map/while/body/eval_jaxpr/dot_general | solution.py:41
  98.3 1.2 dynamic-slice_convert_fusion.2
  99.4 3.4 %fusion.40 = f32[10,2,8,2,32]{4,2,3,1,0:T(8,128)S(1)} fusion(bf16[2,32,18816,1,1]{2,1,0,4,3:T(8,128)(2,1)} %bitcast.110, f32[2,8,18816]{2,1,0:T(8,128)S(1)} %dynamic-slice_convert_fusion.2, f32[10,18816]{1,0:T(8,128)S(1)} %get-tuple-element.192), kind=kOutput, calls=%fused_computation.2.clone.1 | convolution fusion | flops 391372800 | bytes 4406272 | tf_op jit(solution)/shard_map/while/body/eval_jaxpr/dot_general | solution.py:41
  102.9 1.2 dynamic-slice_convert_fusion.2
  104.1 3.4 %fusion.40 = f32[10,2,8,2,32]{4,2,3,1,0:T(8,128)S(1)} fusion(bf16[2,32,18816,1,1]{2,1,0,4,3:T(8,128)(2,1)} %bitcast.110, f32[2,8,18816]{2,1,0:T(8,128)S(1)} %dynamic-slice_convert_fusion.2, f32[10,18816]{1,0:T(8,128)S(1)} %get-tuple-element.192), kind=kOutput, calls=%fused_computation.2.clone.1 | convolution fusion | flops 391372800 | bytes 4406272 | tf_op jit(solution)/shard_map/while/body/eval_jaxpr/dot_general | solution.py:41
  107.6 1.2 dynamic-slice_convert_fusion.2
  108.7 3.4 %fusion.40 = f32[10,2,8,2,32]{4,2,3,1,0:T(8,128)S(1)} fusion(bf16[2,32,18816,1,1]{2,1,0,4,3:T(8,128)(2,1)} %bitcast.110, f32[2,8,18816]{2,1,0:T(8,128)S(1)} %dynamic-slice_convert_fusion.2, f32[10,18816]{1,0:T(8,128)S(1)} %get-tuple-element.192), kind=kOutput, calls=%fused_computation.2.clone.1 | convolution fusion | flops 391372800 | bytes 4406272 | tf_op jit(solution)/shard_map/while/body/eval_jaxpr/dot_general | solution.py:41
  112.2 1.2 dynamic-slice_convert_fusion.2
  113.4 3.4 %fusion.40 = f32[10,2,8,2,32]{4,2,3,1,0:T(8,128)S(1)} fusion(bf16[2,32,18816,1,1]{2,1,0,4,3:T(8,128)(2,1)} %bitcast.110, f32[2,8,18816]{2,1,0:T(8,128)S(1)} %dynamic-slice_convert_fusion.2, f32[10,18816]{1,0:T(8,128)S(1)} %get-tuple-element.192), kind=kOutput, calls=%fused_computation.2.clone.1 | convolution fusion | flops 391372800 | bytes 4406272 | tf_op jit(solution)/shard_map/while/body/eval_jaxpr/dot_general | solution.py:41
  116.9 1.2 dynamic-slice_convert_fusion.2
  118.1 3.4 %fusion.40 = f32[10,2,8,2,32]{4,2,3,1,0:T(8,128)S(1)} fusion(bf16[2,32,18816,1,1]{2,1,0,4,3:T(8,128)(2,1)} %bitcast.110, f32[2,8,18816]{2,1,0:T(8,128)S(1)} %dynamic-slice_convert_fusion.2, f32[10,18816]{1,0:T(8,128)S(1)} %get-tuple-element.192), kind=kOutput, calls=%fused_computation.2.clone.1 | convolution fusion | flops 391372800 | bytes 4406272 | tf_op jit(solution)/shard_map/while/body/eval_jaxpr/dot_general | solution.py:41
  121.6 1.2 dynamic-slice_convert_fusion.2
  122.7 3.4 %fusion.40 = f32[10,2,8,2,32]{4,2,3,1,0:T(8,128)S(1)} fusion(bf16[2,32,18816,1,1]{2,1,0,4,3:T(8,128)(2,1)} %bitcast.110, f32[2,8,18816]{2,1,0:T(8,128)S(1)} %dynamic-slice_convert_fusion.2, f32[10,18816]{1,0:T(8,128)S(1)} %get-tuple-element.192), kind=kOutput, calls=%fused_computation.2.clone.1 | convolution fusion | flops 391372800 | bytes 4406272 | tf_op jit(solution)/shard_map/while/body/eval_jaxpr/dot_general | solution.py:41
  126.2 1.2 dynamic-slice_convert_fusion.2
  127.4 3.4 %fusion.40 = f32[10,2,8,2,32]{4,2,3,1,0:T(8,128)S(1)} fusion(bf16[2,32,18816,1,1]{2,1,0,4,3:T(8,128)(2,1)} %bitcast.110, f32[2,8,18816]{2,1,0:T(8,128)S(1)} %dynamic-slice_convert_fusion.2, f32[10,18816]{1,0:T(8,128)S(1)} %get-tuple-element.192), kind=kOutput, calls=%fused_computation.2.clone.1 | convolution fusion | flops 391372800 | bytes 4406272 | tf_op jit(solution)/shard_map/while/body/eval_jaxpr/dot_general | solution.py:41
  130.9 1.0 copy.27
  131.8 0.0 all-reduce.5.cloned.1.call-update
  131.9 0.0 copy-done
  131.9 0.0 copy-done.1
  131.9 0.2 fusion.10
  132.1 30.9 %all-reduce.5.cloned.1.call-done = f32[32,10,2,64]{3,2,1,0:T(2,128)} async-done(((f32[32,10,2,64]{3,2,1,0:T(2,128)}), f32[32,10,2,64]{3,2,1,0:T(2,128)}) %all-reduce.5.cloned.1.call-update) | async-done | bytes 163856
  163.0 0.9 constant_dynamic-slice_fusion
  163.9 0.3 copy.28
  164.1 0.8 copy.32
  165.0 0.1 copy.29
  165.0 0.1 copy.35
  165.1 0.6 convolution_bitcast_fusion
  165.7 0.4 fusion.13
  166.0 0.4 fusion.17
  166.4 0.1 multiply_reduce_fusion
  166.5 0.1 multiply_reduce_fusion.1
  166.6 5.9 %all-reduce.2 = (f32[3,8]{0,1:T(8,128)S(1)}, f32[6]{0:T(128)S(1)}) all-reduce(f32[3,8]{0,1:T(8,128)S(1)} %multiply_reduce_fusion.1, f32[6]{0:T(128)S(1)} %multiply_reduce_fusion), channel_id=1, replica_groups=mesh['band'=8,'gvec'=4] {'gvec'}, use_global_device_ids=true, to_apply=%region_5.0 | all-reduce | flops 30 | bytes 240 | tf_op jit(solution)/shard_map/psum | solution.py:113
  172.4 21.8 %all-reduce.1 = (f32[3,8]{0,1:T(8,128)S(1)}, f32[6]{0:T(128)S(1)}) all-reduce(f32[3,8]{0,1:T(8,128)S(1)} %get-tuple-element.109, f32[6]{0:T(128)S(1)} %get-tuple-element.110), channel_id=1, replica_groups=mesh['band'=8,'gvec'=4] {'band'}, use_global_device_ids=true, to_apply=%region_6.0 | all-reduce | flops 30 | bytes 240 | tf_op jit(solution)/shard_map/psum | solution.py:113
  194.2 0.7 fusion.28
  194.9 0.1 fusion.29
  194.9 0.7 maximum_bitcast_fusion.3
  195.7 0.5 dynamic-slice_multiply_fusion
  196.2 2.6 %maximum_bitcast_fusion.1 = (f32[1,3]{1,0:T(1,128)S(1)}, f32[1,3]{1,0:T(1,128)S(1)}) fusion(f32[2]{0:T(128)S(1)} %get-tuple-element.137, f32[1]{0:T(128)} %get-tuple-element.132, f32[1]{0:T(128)} %get-tuple-element.134, f32[1]{0:T(128)} %get-tuple-element.135, f32[1]{0:T(128)} %get-tuple-element.136), kind=kLoop, calls=%fused_computation.49 | loop fusion | flops 9 | bytes 48 | tf_op jit(solution)/shard_map/stack | solution.py:75
  198.8 0.6 pad_maximum_fusion
  (27 shorter events, 0.3 us)
Async XLA Ops:
  7.2 124.7 %copy-start = (f32[4,8,8]{2,1,0:T(8,128)S(1)}, f32[4,8,8]{2,1,0:T(8,128)}, u32[]{:S(2)}) copy-start(f32[4,8,8]{2,1,0:T(8,128)} %param.17) | copy-start | bytes 3076
  7.2 86.3 %all-gather.2.cloned.1.call-start = ((), (), s32[]{:S(2)}) async-start(), calls=%async_computation | async-start | bytes 5419008 | tf_op jit(solution)/shard_map/all_gather | solution.py:93
  7.9 155.0 %all-reduce.5.cloned.1.call-start = ((), (), s32[]{:S(2)}) async-start(), calls=%async_computation.1 | async-start | bytes 655360
  93.6 38.3 %copy-start.1 = (s32[8]{0:T(128)S(1)}, s32[8]{0:T(128)}, u32[]{:S(2)}) copy-start(s32[8]{0:T(128)} %param.15) | copy-start | bytes 100
Sparse Core Ops, SparseCore 0:
  10.2 83.2 all-gather.1
  132.0 30.9 all-reduce.4
